TPU v7x, 256 devices: a 8x8x2 block of a 8x8x16 slice. The times are simulated.
256 devices in a mesh: groups: 2 (over z), ep: 16 (over y, core), rep: 8 (over x).
Axes of the slice: x: 8, y: 8, z: 2, core: 2. Of those that a mesh axis runs over, the one named last changes fastest.
The devices are a block of a 8x8x16 slice.
Arguments:
- prompt_hidden: bfloat16 [8, 384, 2048], P('groups', 'ep'), parts along dimension 0, may hold values from -6 to 6
- decode_hidden: bfloat16 [4096, 8, 2048], P(('groups', 'ep'), 'rep'), parts along dimension 0, may hold values from -6 to 6
- queries: bfloat16 [4096, 8, 2048], P(('groups', 'ep'), None, 'rep'), parts along dimension 0, may hold values from -128 to 128
- attn_gain: float32 [2048], replicated, may hold values from 0.1 to 1.9
- key_value_weight: bfloat16 [2048, 1024], P(None, 'rep'), may hold values from -0.125 to 0.125
- out_weight: bfloat16 [2048, 2048], P('rep'), may hold values from -0.5 to 0.5
- moe_gain: float32 [2048], replicated, may hold values from 0.1 to 1.9
- gate_weight: bfloat16 [128, 2048, 768], P(('ep', 'rep')), may hold values from -0.125 to 0.125
- up_weight: bfloat16 [128, 2048, 768], P(('ep', 'rep')), may hold values from -0.125 to 0.125
- down_weight: bfloat16 [128, 768, 2048], P(('ep', 'rep')), may hold values from -0.21875 to 0.21875
- expert_table: int32 [151936], replicated, may hold values from 0 to 127, as said below
- token_ids: int32 [2048, 8], P('ep', 'rep'), may hold values from 0 to 151935, as said below
- prompt_lengths: int32 [8], P('groups'), parts along dimension 0, may hold values from 1 to 384, 960 in all
Outputs:
- layer_out: bfloat16 [4096, 8, 2048], P(('groups', 'ep'), 'rep'), parts along dimension 0
There are 2 independent parts, one for each index of `groups`. A program takes and returns all parts, laid end to end along the dimension named above; an argument that names none is the same for every part. Nothing has to cross between parts.
Inputs may be any that keep to these rules, and one draw needn't show every extreme that they name: `expert_table`: each expert is the value of exactly 1187 entries. `token_ids`: a device holds the 128 sequences of its index of ep at 8 // 8 steps of its index of rep; of these tokens at most 2 go to one expert; in every draw one expert receives exactly 2 from every device. `prompt_lengths`: the lengths of a group sum to 960 and the longest is 384.
All inputs are finite; a program needn't handle non-finite values.
Results may differ from a plain program's by a relative error of at most 0.017.
The roundings to bfloat16 on the way count: a program that leaves them out, or rounds other values in their place, can miss the bound.
Values may be sent and summed in bfloat16 or wider, within the bound.
A program may use at most 128 MiB of HBM per device.

v0:
```python
import math
import jax
import jax.numpy as jnp
from jax import lax
from jax.sharding import PartitionSpec as P

HEAD_DIM = 128
QUERY_HEADS = 16
KEY_VALUE_HEADS = 4
GROUP_PROMPTS = 4
CAP = 2
EPS = 1e-06
THETA = 1000000.0


def in_one_piece(arrays, axis, dim, along):
    both = jnp.concatenate(arrays, axis=along)
    filled, at, outs = (lax.all_gather(both, axis, axis=dim, tiled=True), 0, [])
    for a in arrays:
        outs.append(lax.slice_in_dim(filled, at, at + a.shape[along], axis=along))
        at += a.shape[along]
    return tuple(outs)


def swapped(block, axis, bit):
    count = lax.axis_size(axis)
    route = []
    for low in range(count):
        high = low | 1 << bit
        if high != low and high < count:
            route += [(low, high), (high, low)]
    return lax.ppermute(block, axis, route)


def rms_scale(hidden, gain_vec):
    widened = hidden.astype(jnp.float32)
    mean_sq = jnp.mean(widened * widened, axis=-1, keepdims=True)
    return widened * lax.rsqrt(mean_sq + EPS) * gain_vec


def rotate(vectors, positions):
    half_dim = vectors.shape[-1] // 2
    inverse_freq = jnp.exp(
        jnp.arange(half_dim, dtype=jnp.float32) * (-2.0 * math.log(THETA) / vectors.shape[-1])
    )
    angles = positions[..., None] * inverse_freq
    cosine = jnp.cos(angles)
    sine_part = jnp.sin(angles)
    first_half = vectors[..., :half_dim]
    second_half = vectors[..., half_dim:]
    return jnp.concatenate(
        [
            first_half * cosine - second_half * sine_part,
            second_half * cosine + first_half * sine_part,
        ],
        axis=-1,
    )


def expert_apply(tokens, gate_weight, up_weight, down_weight):
    flat_rows = tokens.reshape(-1, tokens.shape[-1])
    gate_proj = jnp.dot(flat_rows, gate_weight[0], preferred_element_type=jnp.float32)
    up_proj = jnp.dot(flat_rows, up_weight[0], preferred_element_type=jnp.float32)
    hidden = (jax.nn.silu(gate_proj) * up_proj).astype(jnp.bfloat16)
    return (
        jnp.dot(hidden, down_weight[0], preferred_element_type=jnp.float32)
        .astype(jnp.bfloat16)
        .reshape(tokens.shape)
    )


def local(
    prompt_hidden,
    decode_hidden,
    queries,
    attn_gain,
    key_value_weight,
    out_weight,
    moe_gain,
    gate_weight,
    up_weight,
    down_weight,
    expert_table,
    token_ids,
    prompt_lengths,
):
    full_hidden = lax.all_gather(decode_hidden, "rep", axis=1, tiled=True)
    sequences_local, steps_total, model_width = full_hidden.shape
    prompt_length_local = prompt_hidden.shape[1]
    qh_dev = queries.shape[2] // HEAD_DIM
    group_count = QUERY_HEADS // KEY_VALUE_HEADS
    ep_count = lax.axis_size("ep")
    rep_count = lax.axis_size("rep")
    ep_index = lax.axis_index("ep")
    rep_index = lax.axis_index("rep")
    seq_total = sequences_local * ep_count
    samples = seq_total // GROUP_PROMPTS
    score_scale = HEAD_DIM ** (-0.5)
    step_rows = steps_total // rep_count
    blocks = key_value_weight.shape[1] // HEAD_DIM

    def own_columns(hidden, positions):
        leading = hidden.shape[:-1]
        normed = rms_scale(hidden, attn_gain).astype(jnp.bfloat16)
        projected = jnp.dot(
            normed.reshape(-1, model_width), key_value_weight, preferred_element_type=jnp.float32
        )
        projected = projected.reshape(leading + (blocks, HEAD_DIM))
        block_ids = rep_index * blocks + jnp.arange(blocks, dtype=jnp.int32)
        is_key = (block_ids % 2 == 0)[:, None]
        turned = rotate(projected, positions[..., None])
        return (
            jnp.where(is_key, turned, projected)
            .astype(jnp.bfloat16)
            .reshape(leading + (blocks * HEAD_DIM,))
        )

    key_pos = ep_index * prompt_length_local + jnp.arange(prompt_length_local, dtype=jnp.int32)
    prompt_pos = jnp.broadcast_to(
        key_pos.astype(jnp.float32)[None, :], (GROUP_PROMPTS, prompt_length_local)
    )
    own_seqs = ep_index * sequences_local + jnp.arange(sequences_local, dtype=jnp.int32)
    own_prompt = own_seqs // samples
    own_lengths = jnp.take(prompt_lengths, own_prompt)
    decode_pos = (
        own_lengths[:, None].astype(jnp.float32)
        + jnp.arange(steps_total, dtype=jnp.float32)[None, :]
    )
    prompt_part = own_columns(prompt_hidden, prompt_pos)
    decode_part = own_columns(full_hidden, decode_pos)
    prompt_hot = own_prompt[:, None] == jnp.arange(GROUP_PROMPTS, dtype=jnp.int32)[None, :]
    partner_prompt, partner_decode = swapped((prompt_part, decode_part), "rep", 0)
    holds_key = rep_index % 2 == 0
    prompt_columns = jnp.where(
        holds_key,
        jnp.concatenate([prompt_part, partner_prompt], axis=2),
        jnp.concatenate([partner_prompt, prompt_part], axis=2),
    )
    decode_columns = jnp.where(
        holds_key,
        jnp.concatenate([decode_part, partner_decode], axis=2),
        jnp.concatenate([partner_decode, decode_part], axis=2),
    )
    heads_here = 1
    head_base = rep_index // 2
    prompt_key_value = prompt_columns.reshape(
        GROUP_PROMPTS, prompt_length_local, heads_here, 2, HEAD_DIM
    )
    decode_key_value = decode_columns.reshape(sequences_local, steps_total, heads_here, 2, HEAD_DIM)
    prompt_keys = prompt_key_value[:, :, :, 0, :]
    prompt_values = prompt_key_value[:, :, :, 1, :]
    decode_keys = decode_key_value[:, :, :, 0, :]
    decode_values = decode_key_value[:, :, :, 1, :]
    query_matrix = queries.reshape(sequences_local, steps_total, qh_dev, HEAD_DIM)
    head_pick = (
        rep_index * qh_dev + jnp.arange(qh_dev, dtype=jnp.int32)
    ) // group_count - head_base
    own_keys = jnp.take(decode_keys, head_pick, axis=2)
    own_values = jnp.take(decode_values, head_pick, axis=2)
    self_scores = (
        jnp.einsum("sthd,suhd->sthu", query_matrix, own_keys, preferred_element_type=jnp.float32)
        * score_scale
    )
    self_mask = (
        jnp.arange(steps_total, dtype=jnp.int32)[None, :]
        <= jnp.arange(steps_total, dtype=jnp.int32)[:, None]
    )[None, :, None, :]
    self_scores = jnp.where(self_mask, self_scores, -1e30)
    self_top = jnp.max(self_scores, axis=-1)
    start_weights = jnp.where(self_mask, jnp.exp(self_scores - self_top[..., None]), 0.0)
    pieces = in_one_piece((prompt_keys, prompt_values), "ep", 1, 0)
    row_top = self_top
    row_total = jnp.sum(start_weights, axis=-1)
    weighted = jnp.einsum(
        "sthu,suhd->sthd",
        start_weights.astype(jnp.bfloat16),
        own_values,
        preferred_element_type=jnp.float32,
    )
    piece_keys = jnp.take(pieces[0], head_pick, axis=2)
    piece_values = jnp.take(pieces[1], head_pick, axis=2)
    piece_len = piece_keys.shape[1]
    valid = jnp.arange(piece_len, dtype=jnp.int32)[None, :] < prompt_lengths[:, None]
    key_mask = prompt_hot[:, None, None, :, None] & valid[None, None, None, :, :]
    scores = (
        jnp.einsum("sthd,pnhd->sthpn", query_matrix, piece_keys, preferred_element_type=jnp.float32)
        * score_scale
    )
    scores = jnp.where(key_mask, scores, -1e30)
    new_top = jnp.maximum(row_top, jnp.max(scores, axis=(-2, -1)))
    decay = jnp.exp(row_top - new_top)
    weights = jnp.where(key_mask, jnp.exp(scores - new_top[..., None, None]), 0.0)
    weighted = weighted * decay[..., None] + jnp.einsum(
        "sthpn,pnhd->sthd",
        weights.astype(jnp.bfloat16),
        piece_values,
        preferred_element_type=jnp.float32,
    )
    row_top, row_total, weighted = (
        new_top,
        row_total * decay + jnp.sum(weights, axis=(-2, -1)),
        weighted,
    )
    attended = weighted / row_total[..., None]
    heads_out = attended.reshape(sequences_local, steps_total, qh_dev * HEAD_DIM).astype(
        jnp.bfloat16
    )
    by_step = jnp.swapaxes(heads_out, 0, 1)
    attn_sum = jnp.swapaxes(
        lax.psum_scatter(
            jnp.dot(
                by_step.reshape(-1, by_step.shape[-1]),
                out_weight,
                preferred_element_type=jnp.float32,
            )
            .reshape(step_rows * lax.axis_size("rep"), sequences_local, model_width)
            .astype(jnp.bfloat16),
            "rep",
            scatter_dimension=0,
            tiled=True,
        ).astype(jnp.float32),
        0,
        1,
    )
    attn_mixed = (decode_hidden.astype(jnp.float32) + attn_sum).astype(jnp.bfloat16)
    row_count = sequences_local * step_rows
    normed = rms_scale(attn_mixed, moe_gain).astype(jnp.bfloat16).reshape(row_count, model_width)
    chosen = jnp.take(expert_table, token_ids.reshape(row_count))
    device_count = ep_count * rep_count
    slot_total = device_count * CAP
    same_expert = chosen[:, None] == chosen[None, :]
    before = jnp.arange(row_count)[None, :] < jnp.arange(row_count)[:, None]
    slot_rank = jnp.sum((same_expert & before).astype(jnp.int32), axis=1)
    destination = chosen * CAP + slot_rank
    send_pick = (jnp.arange(slot_total, dtype=jnp.int32)[:, None] == destination[None, :]).astype(
        jnp.bfloat16
    )
    outgoing = (
        jnp.dot(send_pick, normed, preferred_element_type=jnp.float32)
        .astype(jnp.bfloat16)
        .reshape(device_count, CAP, model_width)
    )
    served = expert_apply(
        lax.all_to_all(outgoing, ("ep", "rep"), split_axis=0, concat_axis=0, tiled=True),
        gate_weight,
        up_weight,
        down_weight,
    )
    returned = lax.all_to_all(served, ("ep", "rep"), split_axis=0, concat_axis=0, tiled=True)
    moe_out = lax.dot_general(
        send_pick,
        returned.reshape(slot_total, model_width),
        (((0,), (0,)), ((), ())),
        preferred_element_type=jnp.float32,
    )
    layer_out = (
        attn_mixed.astype(jnp.float32) + moe_out.reshape(sequences_local, step_rows, model_width)
    ).astype(jnp.bfloat16)
    return layer_out


def solution(mesh):
    placed = (
        P("groups", "ep", None),
        P(("groups", "ep"), "rep", None),
        P(("groups", "ep"), None, "rep"),
        P(),
        P(None, "rep"),
        P("rep", None),
        P(),
        P(("ep", "rep"), None, None),
        P(("ep", "rep"), None, None),
        P(("ep", "rep"), None, None),
        P(),
        P("ep", "rep"),
        P("groups"),
    )
    return jax.shard_map(
        local,
        mesh=mesh,
        in_specs=placed,
        out_specs=P(("groups", "ep"), "rep", None),
        check_vma=False,
    )
```

profile of v0, /device:TPU:513, one launch (start us, length us, event | category | flops | bytes accessed | tf_op | source)
XLA Modules:
  0.0 316.9 jit_solution(7113456730417869289)
XLA Ops:
  11.4 2.3 collective-permute-start.1
  15.1 2.5 fusion.100
  21.3 35.0 %all_gather.7 = bf16[8,384,1,128]{3,0,2,1:T(8,128)(2,1)S(1)} all-gather(bf16[8,24,1,128]{3,0,2,1:T(8,128)(2,1)S(1)} %copy.139), channel_id=1, replica_groups=mesh['groups'=2,'ep'=16,'rep'=8] {'ep'}, dimensions={1}, use_global_device_ids=true | all-gather | bytes 835584 | tf_op jit(solution)/shard_map/all_gather | solution.py:18
  57.3 26.0 %all-gather.2.cloned.1.call-done = bf16[128,8,2048]{2,0,1:T(8,128)(2,1)} async-done(((bf16[128,1,2048]{2,0,1:T(8,128)(2,1)}), bf16[128,8,2048]{2,0,1:T(8,128)(2,1)}) %all-gather.2.cloned.1.call-update) | async-done | bytes 4194320 | tf_op jit(solution)/shard_map/all_gather | solution.py:87
  83.4 5.1 %fusion.3 = f32[128,8]{1,0:T(8,128)} fusion(bf16[128,8,2048]{2,0,1:T(8,128)(2,1)} %all-gather.2.cloned.1.call-done), kind=kLoop, calls=%fused_computation.8 | loop fusion | flops 6290432 | bytes 4198400 | tf_op jit(solution)/shard_map/reduce_sum | solution.py:37
  90.2 5.0 %fusion.7 = f32[1024,128]{1,0:T(8,128)S(1)} fusion(bf16[2048,128]{1,0:T(8,128)(2,1)} %param.21, f32[2048]{0:T(1024)S(1)} %copy-done.10, f32[128,8]{1,0:T(8,128)} %copy.132, bf16[128,8,2048]{2,0,1:T(8,128)(2,1)} %all-gather.2.cloned.1.call-done), kind=kOutput, calls=%fused_computation.12 | convolution fusion | flops 545259520 | bytes 5255168 | tf_op jit(solution)/shard_map/dot_general | solution.py:105
  95.2 2.4 fusion.56
  98.1 5.7 %fusion = (f32[128,8,2]{0,1,2:T(8,128)S(1)}, f32[2,4,384,128,8]{3,2,4,1,0:T(8,128)}) fusion(pred[128,4,384]{0,2,1:T(8,128)(4,1)S(1)} %copy-done.3, bf16[128,8,2,128,1]{3,1,2,0,4:T(8,128)(2,1)S(1)} %bitcast.168, pred[2]{0:T(512)(128)(4,1)S(1)} %copy-done.14, bf16[4,384,128]{2,1,0:T(8,128)(2,1)S(1)} %copy-done.6), kind=kOutput, calls=%fused_computation.3 | convolution fusion | flops 815134720 | bytes 13705218 | tf_op jit(solution)/shard_map/sthd,pnhd->sthpn/dot_general | solution.py:186
  111.8 9.7 %fusion.2 = (bf16[128,8,2,4,384]{0,4,1,3,2:T(8,128)(2,1)}, f32[128,8,2]{0,1,2:T(8,128)S(1)}) fusion(f32[2,4,384,128,8]{3,2,4,1,0:T(8,128)} %get-tuple-element.28, f32[128,8,2]{0,1,2:T(8,128)S(1)} %copy_maximum_fusion, pred[128,4,384]{0,2,1:T(8,128)(4,1)} %broadcast_and_fusion), kind=kLoop, calls=%fused_computation.7 | loop fusion | flops 18872320 | bytes 19087360 | tf_op jit(solution)/shard_map/convert_element_type | solution.py:195
  121.5 9.0 %copy.146 = bf16[128,8,2,4,384]{4,1,3,2,0:T(8,128)(2,1)} copy(bf16[128,8,2,4,384]{0,4,1,3,2:T(8,128)(2,1)} %get-tuple-element.9) | data formatting | bytes 12582912 | tf_op jit(solution)/shard_map/convert_element_type | solution.py:195
  139.9 2.6 fusion.33
  142.6 3.2 %convolution_convert_fusion = bf16[8,128,2048]{2,1,0:T(8,128)(2,1)} fusion(bf16[256,2048]{1,0:T(8,128)(2,1)S(1)} %copy-done.2, bf16[8,128,256]{2,0,1:T(8,128)(2,1)S(1)} %fusion.33), kind=kOutput, calls=%fused_computation.15 | convolution fusion | flops 1075838976 | bytes 5767168 | tf_op jit(solution)/shard_map/dot_general | solution.py:211
  145.9 2.1 gather_fusion
  148.2 54.3 %reduce-scatter.2.cloned.1.call-done = bf16[1,128,2048]{2,1,0:T(8,128)(2,1)} async-done(((bf16[8,128,2048]{2,1,0:T(8,128)(2,1)}), bf16[1,128,2048]{2,1,0:T(8,128)(2,1)}) %reduce-scatter.2.cloned.1.call-update) | async-done | bytes 524304 | tf_op jit(solution)/shard_map/reduce_scatter | solution.py:210
  203.9 2.7 convolution_convert_fusion.1
  206.7 2.5 reshape.407
  209.2 42.8 %all_to_all.10 = bf16[128,2,2048]{2,1,0:T(2,128)(2,1)} all-to-all(bf16[128,2,2048]{2,1,0:T(2,128)(2,1)} %reshape.407), channel_id=1, replica_groups=mesh['groups'=2,'ep'=16,'rep'=8] {'ep','rep'}, dimensions={0} | all-to-all | bytes 2097152 | tf_op jit(solution)/shard_map/all_to_all | solution.py:244
  252.0 2.2 reshape.408
  254.3 4.1 %fusion.16 = f32[256,768]{1,0:T(8,128)} fusion(bf16[256,2048]{1,0:T(8,128)(2,1)} %reshape.408, bf16[1,2048,768]{2,1,0:T(8,128)(2,1)} %param.24), kind=kOutput, calls=%fused_computation.21 | convolution fusion | flops 805306368 | bytes 4980736 | tf_op jit(solution)/shard_map/dot_general | solution.py:62
  258.3 5.5 %fusion.18 = bf16[256,2048]{1,0:T(8,128)(2,1)} fusion(bf16[1,768,2048]{2,1,0:T(8,128)(2,1)S(1)} %copy-done, bf16[256,2048]{1,0:T(8,128)(2,1)} %reshape.408, bf16[1,2048,768]{2,1,0:T(8,128)(2,1)} %param.25, f32[256,768]{1,0:T(8,128)} %fusion.16), kind=kOutput, calls=%fused_computation.24 | convolution fusion | flops 1612316672 | bytes 9175040 | tf_op jit(solution)/shard_map/dot_general | solution.py:66
  263.9 2.5 reshape.409
  266.4 38.7 %all_to_all.11 = bf16[128,2,2048]{2,1,0:T(2,128)(2,1)} all-to-all(bf16[128,2,2048]{2,1,0:T(2,128)(2,1)} %reshape.409), channel_id=1, replica_groups=mesh['groups'=2,'ep'=16,'rep'=8] {'ep','rep'}, dimensions={0} | all-to-all | bytes 2097152 | tf_op jit(solution)/shard_map/all_to_all | solution.py:249
  305.1 2.2 reshape.410
  307.3 2.7 fusion.22
  (88 shorter events, 32.1 us)
Async XLA Ops:
  6.5 251.8 %copy-start = (bf16[1,768,2048]{2,1,0:T(8,128)(2,1)S(1)}, bf16[1,768,2048]{2,1,0:T(8,128)(2,1)}, u32[]{:S(2)}) copy-start(bf16[1,768,2048]{2,1,0:T(8,128)(2,1)} %param.26) | copy-start | bytes 9437188
  6.6 83.6 %copy-start.10 = (f32[2048]{0:T(1024)S(1)}, f32[2048]{0:T(1024)}, u32[]{:S(2)}) copy-start(f32[2048]{0:T(1024)} %param.20) | copy-start | bytes 24580
  6.6 76.8 %all-gather.2.cloned.1.call-start = ((), (), s32[]{:S(2)}) async-start(), calls=%async_computation.3 | async-start | bytes 4718592 | tf_op jit(solution)/shard_map/all_gather | solution.py:87
  7.3 195.2 %reduce-scatter.2.cloned.1.call-start = ((), (), s32[]{:S(2)}) async-start(), calls=%async_computation.4 | async-start | bytes 4718592 | tf_op jit(solution)/shard_map/reduce_scatter | solution.py:210
  7.4 4.0 %copy-start.12 = (f32[64]{0:T(128)}, f32[64]{0:T(128)S(1)}, u32[]{:S(2)}) copy-start(f32[64]{0:T(128)S(1)} %multiply_exponential_fusion) | copy-start | bytes 772
  11.4 9.7 %collective-permute-start.1 = (bf16[4,24,128]{2,1,0:T(8,128)(2,1)S(1)}, bf16[4,24,128]{2,1,0:T(8,128)(2,1)S(1)}, u32[]{:S(2)}, u32[]{:S(2)}) collective-permute-start(bf16[4,24,128]{2,1,0:T(8,128)(2,1)S(1)} %fusion.94), channel_id=1, source_target_pairs={{0,1},{1,0},{2,3},{3,2},{4,5},{5,4},{6,7},{7,6},{8,9},{9,8},{10,11... | collective-permute-start | bytes 73736 | tf_op jit(solution)/shard_map/ppermute | solution.py:32
  90.2 5.0 %copy-start.7 = (f32[128,8]{1,0:T(8,128)S(1)}, f32[128,8]{1,0:T(8,128)}, u32[]{:S(2)}) copy-start(f32[128,8]{1,0:T(8,128)} %iota_add_fusion) | copy-start | bytes 12292
  90.2 5.0 %copy-start.13 = (f32[64]{0:T(128)S(1)}, f32[64]{0:T(128)}, u32[]{:S(2)}) copy-start(f32[64]{0:T(128)} %copy-done.12) | copy-start | bytes 772
  90.2 7.9 %copy-start.3 = (pred[128,4,384]{0,2,1:T(8,128)(4,1)S(1)}, pred[128,4,384]{0,2,1:T(8,128)(4,1)}, u32[]{:S(2)}) copy-start(pred[128,4,384]{0,2,1:T(8,128)(4,1)} %broadcast_and_fusion) | copy-start | bytes 589828
  90.2 7.9 %copy-start.4 = (bf16[128,8,256]{2,1,0:T(8,128)(2,1)S(1)}, bf16[128,8,256]{2,1,0:T(8,128)(2,1)}, u32[]{:S(2)}) copy-start(bf16[128,8,256]{2,1,0:T(8,128)(2,1)} %param.19) | copy-start | bytes 1572868
  90.2 7.9 %copy-start.6 = (bf16[4,384,128]{2,1,0:T(8,128)(2,1)S(1)}, bf16[4,384,128]{2,1,0:T(8,128)(2,1)}, u32[]{:S(2)}) copy-start(bf16[4,384,128]{2,1,0:T(8,128)(2,1)} %copy.140) | copy-start | bytes 1179652
  90.2 7.9 %copy-start.14 = (pred[2]{0:T(512)(128)(4,1)S(1)}, pred[2]{0:T(512)(128)(4,1)}, u32[]{:S(2)}) copy-start(pred[2]{0:T(512)(128)(4,1)} %compare_and_fusion) | copy-start | bytes 10
  97.8 7.3 %collective-permute-start = (bf16[128,8,128]{2,1,0:T(8,128)(2,1)S(1)}, bf16[128,8,128]{2,1,0:T(8,128)(2,1)S(1)}, u32[]{:S(2)}, u32[]{:S(2)}) collective-permute-start(bf16[128,8,128]{2,1,0:T(8,128)(2,1)S(1)} %fusion.61), channel_id=1, source_target_pairs={{0,1},{1,0},{2,3},{3,2},{4,5},{5,4},{6,7},{7,6},{8,9},{9,8},{10,11... | collective-permute-start | bytes 786440 | tf_op jit(solution)/shard_map/ppermute | solution.py:32
  103.8 8.0 %copy-start.9 = (f32[128,8,2]{0,1,2:T(8,128)}, f32[128,8,2]{0,1,2:T(8,128)S(1)}, u32[]{:S(2)}) copy-start(f32[128,8,2]{0,1,2:T(8,128)S(1)} %get-tuple-element.27) | copy-start | bytes 24580
  130.6 8.1 %copy-start.5 = (bf16[4,384,128]{2,1,0:T(8,128)(2,1)S(1)}, bf16[4,384,128]{2,1,0:T(8,128)(2,1)}, u32[]{:S(2)}) copy-start(bf16[4,384,128]{2,1,0:T(8,128)(2,1)} %copy.145) | copy-start | bytes 1179652
  136.8 3.1 copy-start.1
  136.8 3.1 copy-start.8
  139.9 2.6 copy-start.2
  142.6 3.3 %copy-start.15 = (s32[128,1]{0,1:T(1,128)S(1)}, s32[128,1]{0,1:T(1,128)}, u32[]{:S(2)}) copy-start(s32[128,1]{0,1:T(1,128)} %param.28) | copy-start | bytes 1540
  142.6 61.4 %copy-start.11 = (f32[2048]{0:T(1024)S(1)}, f32[2048]{0:T(1024)}, u32[]{:S(2)}) copy-start(f32[2048]{0:T(1024)} %param.23) | copy-start | bytes 24580
Sparse Core Ops, SparseCore 0:
  9.1 74.2 all-gather.1
  146.0 56.4 reduce-scatter.1
where the time goes:
time: 318 us; the launch traced here: 317 us
  blocking collectives  116 us (36%)
  waiting for transfers between devices  81.6 us (26%)
  matrix products  36.1 us (11%)
  local copies, waits for them, and re-layouts  34.3 us (11%)
  other arithmetic  31.9 us (10%)
  between operations  13.8 us (4%)
    reduce_scatter x1, waiting for transfers between devices, local(): lax.psum_scatter(jnp.dot(by_step.reshape(-1, by_step.shape[-1]), out_weig...  54.3 us
    all_to_all x1, blocking collectives, local(): lax.all_to_all(outgoing, ('ep', 'rep'), split_axis=0, concat_axis=0, tile...  42.8 us
    all_to_all x1, blocking collectives, local(): lax.all_to_all(served, ('ep', 'rep'), split_axis=0, concat_axis=0, tiled=...  38.7 us
    all_gather x1, blocking collectives, in_one_piece(): filled, at, outs = (lax.all_gather(both, axis, axis=dim, tiled=True), 0, [])  35 us
    all_gather x1, waiting for transfers between devices, local(): full_hidden = lax.all_gather(decode_hidden, 'rep', axis=1, tiled=True)  26 us
    convert_element_type x1, other arithmetic, local(): weights.astype(jnp.bfloat16)  9.72 us
    convert_element_type x1, local copies, waits for them, and re-layouts, local(): weights.astype(jnp.bfloat16)  9.02 us
    reduce_sum x3, other arithmetic, rms_scale(): mean_sq = jnp.mean(widened * widened, axis=-1, keepdims=True)  7.81 us
  transfers between devices with their start and end apart: 4, of which 3 were waited for; matrix products, arithmetic and copies ran while one was open for 7% of the time, Pallas kernels for 0%

commit v1 on v0

--- a/solution.py
+++ b/solution.py
@@ -3,6 +3,7 @@
 import jax.numpy as jnp
 from jax import lax
 from jax.sharding import PartitionSpec as P
+from jax.lax import all_to_all, axis_size
 
 HEAD_DIM = 128
 QUERY_HEADS = 16
@@ -84,7 +85,12 @@
     token_ids,
     prompt_lengths,
 ):
-    full_hidden = lax.all_gather(decode_hidden, "rep", axis=1, tiled=True)
+    full_hidden = jnp.concatenate(
+        all_to_all(
+            jnp.stack([decode_hidden for _ in range(axis_size("rep"))], axis=0), "rep", 0, 0
+        ),
+        axis=1,
+    )
     sequences_local, steps_total, model_width = full_hidden.shape
     prompt_length_local = prompt_hidden.shape[1]
     qh_dev = queries.shape[2] // HEAD_DIM

time: 318 us -> 376 us (1.18)
  waiting for transfers between devices: 81.6 us -> 129 us
  blocking collectives: 116 us -> 126 us
  starting transfers between devices: 2.67 us -> 9.87 us
  other arithmetic: 31.9 us -> 25.5 us
    ppermute x2, waiting for transfers between devices: 0.47 us -> 68.7 us  [swapped(): return lax.ppermute(block, axis, route)]
    all_gather x1 -> x0, waiting for transfers between devices: 26 us -> none  [local(): full_hidden = lax.all_gather(decode_hidden, 'rep', axis=1, tiled=True)]
    all_gather x1, blocking collectives: 35 us -> 44.4 us  [in_one_piece(): filled, at, outs = (lax.all_gather(both, axis, axis=dim, tiled=True), 0, [])]
    all_to_all x0 -> x1, starting transfers between devices: none -> 7.99 us  [local(): all_to_all(jnp.stack([decode_hidden for _ in range(axis_size('rep'))], ax...]
    reduce_scatter x1, waiting for transfers between devices: 54.3 us -> 60.2 us  [local(): lax.psum_scatter(jnp.dot(by_step.reshape(-1, by_step.shape[-1]), out_weig...]
  transfers between devices with their start and end apart: 4 -> 4, of which waited for: 3 -> 3; matrix products, arithmetic and copies ran while one was open for 7% -> 5% of each run, Pallas kernels for 0% -> 0%
where the time goes in v1:
time: 376 us; the launch traced here: 375 us
  waiting for transfers between devices  129 us (34%)
  blocking collectives  126 us (34%)
  local copies, waits for them, and re-layouts  35.9 us (10%)
  matrix products  35.6 us (9%)
  other arithmetic  25.5 us (7%)
  between operations  13.8 us (4%)
  starting transfers between devices  9.87 us (3%)
    ppermute x2, waiting for transfers between devices, swapped(): return lax.ppermute(block, axis, route)  68.7 us
    reduce_scatter x1, waiting for transfers between devices, local(): lax.psum_scatter(jnp.dot(by_step.reshape(-1, by_step.shape[-1]), out_weig...  60.2 us
    all_gather x1, blocking collectives, in_one_piece(): filled, at, outs = (lax.all_gather(both, axis, axis=dim, tiled=True), 0, [])  44.4 us
    all_to_all x1, blocking collectives, local(): lax.all_to_all(outgoing, ('ep', 'rep'), split_axis=0, concat_axis=0, tile...  42.8 us
    all_to_all x1, blocking collectives, local(): lax.all_to_all(served, ('ep', 'rep'), split_axis=0, concat_axis=0, tiled=...  38.7 us
    convert_element_type x1, other arithmetic, local(): weights.astype(jnp.bfloat16)  9.69 us
    convert_element_type x1, local copies, waits for them, and re-layouts, local(): weights.astype(jnp.bfloat16)  8.98 us
    all_to_all x1, starting transfers between devices, local(): all_to_all(jnp.stack([decode_hidden for _ in range(axis_size('rep'))], ax...  7.99 us
  transfers between devices with their start and end apart: 4, of which 3 were waited for; matrix products, arithmetic and copies ran while one was open for 5% of the time, Pallas kernels for 0%

profile of v1, /device:TPU:513, one launch (start us, length us, event | category | flops | bytes accessed | tf_op | source)
XLA Modules:
  0.0 375.5 jit_solution(16706068130267029751)
XLA Ops:
  6.6 3.7 stack.2
  10.2 8.0 %all-to-all-start = ((bf16[8,128,1,2048]{3,1,2,0:T(8,128)(2,1)}), bf16[8,128,1,2048]{3,1,2,0:T(8,128)(2,1)}, u32[]{:S(2)}, u32[]{:S(2)}) async-start(bf16[8,128,1,2048]{3,1,2,0:T(8,128)(2,1)} %stack.2), calls=%async_computation | async-start | bytes 8388608 | tf_op jit(solution)/shard_map/all_to_all | solution.py:89
  22.4 2.5 fusion.100
  27.9 67.7 %collective-permute-done.1 = bf16[4,24,128]{2,1,0:T(8,128)(2,1)S(1)} collective-permute-done((bf16[4,24,128]{2,1,0:T(8,128)(2,1)S(1)}, bf16[4,24,128]{2,1,0:T(8,128)(2,1)S(1)}, u32[]{:S(2)}, u32[]{:S(2)}) %collective-permute-start.1) | collective-permute-done | bytes 24608 | tf_op jit(solution)/shard_map/ppermute | solution.py:33
  95.8 44.4 %all_gather.3 = bf16[8,384,1,128]{3,0,2,1:T(8,128)(2,1)S(1)} all-gather(bf16[8,24,1,128]{3,0,2,1:T(8,128)(2,1)S(1)} %copy.138), channel_id=1, replica_groups=mesh['groups'=2,'ep'=16,'rep'=8] {'ep'}, dimensions={1}, use_global_device_ids=true | all-gather | bytes 835584 | tf_op jit(solution)/shard_map/all_gather | solution.py:19
  141.2 5.1 %fusion.6 = f32[8,128]{0,1:T(8,128)} fusion(bf16[8,128,1,2048]{3,1,2,0:T(8,128)(2,1)} %all-to-all-done), kind=kLoop, calls=%fused_computation.11 | loop fusion | flops 6290432 | bytes 4198400 | tf_op jit(solution)/shard_map/reduce_sum | solution.py:38
  149.0 4.9 %fusion.7 = f32[1024,128]{1,0:T(8,128)S(1)} fusion(bf16[2048,128]{1,0:T(8,128)(2,1)} %param.21, f32[2048]{0:T(1024)S(1)} %copy-done.11, f32[1024]{0:T(1024)S(1)} %rsqrt.28, bf16[8,128,1,2048]{3,1,2,0:T(8,128)(2,1)} %all-to-all-done), kind=kOutput, calls=%fused_computation.12 | convolution fusion | flops 545259520 | bytes 5255168 | tf_op jit(solution)/shard_map/dot_general | solution.py:111
  154.0 2.4 fusion.56
  156.9 5.8 %fusion = (f32[128,8,2]{0,1,2:T(8,128)S(1)}, f32[2,4,384,128,8]{3,2,4,1,0:T(8,128)}) fusion(pred[128,4,384]{0,2,1:T(8,128)(4,1)S(1)} %copy-done.4, bf16[128,8,2,128,1]{3,1,2,0,4:T(8,128)(2,1)S(1)} %bitcast.180, pred[2]{0:T(512)(128)(4,1)S(1)} %copy-done.16, bf16[4,384,128]{2,1,0:T(8,128)(2,1)S(1)} %copy-done.7), kind=kOutput, calls=%fused_computation.3 | convolution fusion | flops 815134720 | bytes 13705218 | tf_op jit(solution)/shard_map/sthd,pnhd->sthpn/dot_general | solution.py:192
  170.0 9.7 %fusion.2 = (bf16[128,8,2,4,384]{0,4,1,3,2:T(8,128)(2,1)}, f32[128,8,2]{0,1,2:T(8,128)S(1)}) fusion(f32[2,4,384,128,8]{3,2,4,1,0:T(8,128)} %get-tuple-element.28, f32[128,8,2]{0,1,2:T(8,128)S(1)} %copy_maximum_fusion, pred[128,4,384]{0,2,1:T(8,128)(4,1)} %broadcast_and_fusion), kind=kLoop, calls=%fused_computation.7 | loop fusion | flops 18872320 | bytes 19087360 | tf_op jit(solution)/shard_map/convert_element_type | solution.py:201
  180.5 9.0 %copy.145 = bf16[128,8,2,4,384]{4,1,3,2,0:T(8,128)(2,1)} copy(bf16[128,8,2,4,384]{0,4,1,3,2:T(8,128)(2,1)} %get-tuple-element.9) | data formatting | bytes 12582912 | tf_op jit(solution)/shard_map/convert_element_type | solution.py:201
  195.4 3.2 convolution_convert_fusion
  198.7 2.1 gather_fusion
  201.0 60.2 %reduce-scatter.2.cloned.1.call-done = bf16[1,128,2048]{2,1,0:T(8,128)(2,1)} async-done(((bf16[8,128,2048]{2,1,0:T(8,128)(2,1)}), bf16[1,128,2048]{2,1,0:T(8,128)(2,1)}) %reduce-scatter.2.cloned.1.call-update) | async-done | bytes 524304 | tf_op jit(solution)/shard_map/reduce_scatter | solution.py:216
  262.6 2.7 convolution_convert_fusion.1
  265.4 2.5 reshape.422
  267.9 42.8 %all_to_all.15 = bf16[128,2,2048]{2,1,0:T(2,128)(2,1)} all-to-all(bf16[128,2,2048]{2,1,0:T(2,128)(2,1)} %reshape.422), channel_id=1, replica_groups=mesh['groups'=2,'ep'=16,'rep'=8] {'ep','rep'}, dimensions={0} | all-to-all | bytes 2097152 | tf_op jit(solution)/shard_map/all_to_all | solution.py:250
  310.7 2.2 reshape.423
  312.9 4.1 %fusion.16 = f32[256,768]{1,0:T(8,128)} fusion(bf16[256,2048]{1,0:T(8,128)(2,1)} %reshape.423, bf16[1,2048,768]{2,1,0:T(8,128)(2,1)} %param.24), kind=kOutput, calls=%fused_computation.21 | convolution fusion | flops 805306368 | bytes 4980736 | tf_op jit(solution)/shard_map/dot_general | solution.py:63
  317.0 5.5 %fusion.18 = bf16[256,2048]{1,0:T(8,128)(2,1)} fusion(bf16[1,768,2048]{2,1,0:T(8,128)(2,1)S(1)} %copy-done, bf16[256,2048]{1,0:T(8,128)(2,1)} %reshape.423, bf16[1,2048,768]{2,1,0:T(8,128)(2,1)} %param.25, f32[256,768]{1,0:T(8,128)} %fusion.16), kind=kOutput, calls=%fused_computation.24 | convolution fusion | flops 1612316672 | bytes 9175040 | tf_op jit(solution)/shard_map/dot_general | solution.py:67
  322.5 2.5 reshape.424
  325.1 38.7 %all_to_all.16 = bf16[128,2,2048]{2,1,0:T(2,128)(2,1)} all-to-all(bf16[128,2,2048]{2,1,0:T(2,128)(2,1)} %reshape.424), channel_id=1, replica_groups=mesh['groups'=2,'ep'=16,'rep'=8] {'ep','rep'}, dimensions={0} | all-to-all | bytes 2097152 | tf_op jit(solution)/shard_map/all_to_all | solution.py:255
  363.7 2.2 reshape.425
  366.0 2.7 fusion.22
  (95 shorter events, 26.9 us)
Async XLA Ops:
  6.5 310.5 %copy-start = (bf16[1,768,2048]{2,1,0:T(8,128)(2,1)S(1)}, bf16[1,768,2048]{2,1,0:T(8,128)(2,1)}, u32[]{:S(2)}) copy-start(bf16[1,768,2048]{2,1,0:T(8,128)(2,1)} %param.26) | copy-start | bytes 9437188
  6.6 11.8 %copy-start.2 = (bf16[4,24,2048]{2,1,0:T(8,128)(2,1)S(1)}, bf16[4,24,2048]{2,1,0:T(8,128)(2,1)}, u32[]{:S(2)}) copy-start(bf16[4,24,2048]{2,1,0:T(8,128)(2,1)} %param.17) | copy-start | bytes 1179652
  6.6 12.0 %copy-start.11 = (f32[2048]{0:T(1024)S(1)}, f32[2048]{0:T(1024)}, u32[]{:S(2)}) copy-start(f32[2048]{0:T(1024)} %param.20) | copy-start | bytes 24580
  10.2 11.5 %copy-start.10 = (s32[4]{0:T(128)S(1)}, s32[4]{0:T(128)}, u32[]{:S(2)}) copy-start(s32[4]{0:T(128)} %param.29) | copy-start | bytes 52
  10.2 131.0 %all-to-all-start = ((bf16[8,128,1,2048]{3,1,2,0:T(8,128)(2,1)}), bf16[8,128,1,2048]{3,1,2,0:T(8,128)(2,1)}, u32[]{:S(2)}, u32[]{:S(2)}) async-start(bf16[8,128,1,2048]{3,1,2,0:T(8,128)(2,1)} %stack.2), calls=%async_computation | async-start | bytes 8388608 | tf_op jit(solution)/shard_map/all_to_all | solution.py:89
  18.2 242.9 %reduce-scatter.2.cloned.1.call-start = ((), (), s32[]{:S(2)}) async-start(), calls=%async_computation.4 | async-start | bytes 4718592 | tf_op jit(solution)/shard_map/reduce_scatter | solution.py:216
  18.3 1.9 copy-start.14
  20.3 75.3 %collective-permute-start.1 = (bf16[4,24,128]{2,1,0:T(8,128)(2,1)S(1)}, bf16[4,24,128]{2,1,0:T(8,128)(2,1)S(1)}, u32[]{:S(2)}, u32[]{:S(2)}) collective-permute-start(bf16[4,24,128]{2,1,0:T(8,128)(2,1)S(1)} %fusion.94), channel_id=1, source_target_pairs={{0,1},{1,0},{2,3},{3,2},{4,5},{5,4},{6,7},{7,6},{8,9},{9,8},{10,11... | collective-permute-start | bytes 73736 | tf_op jit(solution)/shard_map/ppermute | solution.py:33
  148.9 5.0 %copy-start.8 = (f32[128,8]{1,0:T(8,128)S(1)}, f32[128,8]{1,0:T(8,128)}, u32[]{:S(2)}) copy-start(f32[128,8]{1,0:T(8,128)} %iota_add_fusion) | copy-start | bytes 12292
  149.0 5.0 %copy-start.15 = (f32[64]{0:T(128)S(1)}, f32[64]{0:T(128)}, u32[]{:S(2)}) copy-start(f32[64]{0:T(128)} %copy-done.14) | copy-start | bytes 772
  149.0 7.9 %copy-start.4 = (pred[128,4,384]{0,2,1:T(8,128)(4,1)S(1)}, pred[128,4,384]{0,2,1:T(8,128)(4,1)}, u32[]{:S(2)}) copy-start(pred[128,4,384]{0,2,1:T(8,128)(4,1)} %broadcast_and_fusion) | copy-start | bytes 589828
  149.0 7.9 %copy-start.5 = (bf16[128,8,256]{2,1,0:T(8,128)(2,1)S(1)}, bf16[128,8,256]{2,1,0:T(8,128)(2,1)}, u32[]{:S(2)}) copy-start(bf16[128,8,256]{2,1,0:T(8,128)(2,1)} %param.19) | copy-start | bytes 1572868
  149.0 7.9 %copy-start.7 = (bf16[4,384,128]{2,1,0:T(8,128)(2,1)S(1)}, bf16[4,384,128]{2,1,0:T(8,128)(2,1)}, u32[]{:S(2)}) copy-start(bf16[4,384,128]{2,1,0:T(8,128)(2,1)} %copy.139) | copy-start | bytes 1179652
  149.0 7.9 %copy-start.16 = (pred[2]{0:T(512)(128)(4,1)S(1)}, pred[2]{0:T(512)(128)(4,1)}, u32[]{:S(2)}) copy-start(pred[2]{0:T(512)(128)(4,1)} %compare_and_fusion) | copy-start | bytes 10
  156.5 8.0 %collective-permute-start = (bf16[128,8,128]{2,1,0:T(8,128)(2,1)S(1)}, bf16[128,8,128]{2,1,0:T(8,128)(2,1)S(1)}, u32[]{:S(2)}, u32[]{:S(2)}) collective-permute-start(bf16[128,8,128]{2,1,0:T(8,128)(2,1)S(1)} %fusion.61), channel_id=1, source_target_pairs={{0,1},{1,0},{2,3},{3,2},{4,5},{5,4},{6,7},{7,6},{8,9},{9,8},{10,11... | collective-permute-start | bytes 786440 | tf_op jit(solution)/shard_map/ppermute | solution.py:33
  156.9 11.7 %copy-start.13 = (pred[8,8]{1,0:T(8,128)(4,1)S(1)}, pred[8,8]{1,0:T(8,128)(4,1)}, u32[]{:S(2)}) copy-start(pred[8,8]{1,0:T(8,128)(4,1)} %iota_compare_fusion.5) | copy-start | bytes 196
  180.5 9.8 %copy-start.17 = (pred[2]{0:T(512)(128)(4,1)S(1)}, pred[2]{0:T(512)(128)(4,1)}, u32[]{:S(2)}) copy-start(pred[2]{0:T(512)(128)(4,1)} %compare_and_fusion) | copy-start | bytes 10
  189.5 2.6 copy-start.6
  190.3 3.1 copy-start.1
  190.3 3.1 copy-start.9
  193.4 1.9 copy-start.3
  195.3 3.3 copy-start.18
  195.3 67.3 %copy-start.12 = (f32[2048]{0:T(1024)S(1)}, f32[2048]{0:T(1024)}, u32[]{:S(2)}) copy-start(f32[2048]{0:T(1024)} %param.23) | copy-start | bytes 24580
Sparse Core Ops, SparseCore 0:
  198.8 62.3 reduce-scatter.1
